TPU v7x, 32 devices: a whole 2x2x4 slice. The times are simulated.
32 devices in a mesh: rep: 8 (over y, x, core), fsdp: 4 (over z).
Axes of the slice: x: 2, y: 2, z: 4, core: 2. Of those that a mesh axis runs over, the one named last changes fastest.
Arguments:
- tokens: bfloat16 [16384, 768], P(('rep', 'fsdp')), may hold values from -6 to 6
- cotangent: bfloat16 [16384, 768], P(('rep', 'fsdp')), may hold values from -6 to 6
- lengths: int32 [32], P(('rep', 'fsdp')), may hold values from 1 to 512, 10240 in all
- slot_seq: int32 [32], replicated, may hold values from 0 to 31, each once
- query_weight: bfloat16 [768, 768], P('fsdp'), may hold values from -0.21875 to 0.21875
- query_bias: bfloat16 [768], P('fsdp'), may hold values from -2 to 2
- key_weight: bfloat16 [768, 768], P('fsdp'), may hold values from -0.21875 to 0.21875
- value_weight: bfloat16 [768, 768], P('fsdp'), may hold values from -0.21875 to 0.21875
- value_bias: bfloat16 [768], P('fsdp'), may hold values from -2 to 2
- out_weight: bfloat16 [768, 768], P('fsdp'), may hold values from -2.5 to 2.5
- out_bias: bfloat16 [768], P('fsdp'), may hold values from -2 to 2
- first_gain: bfloat16 [768], P('fsdp'), may hold values from 0.5 to 1.5
- first_shift: bfloat16 [768], P('fsdp'), may hold values from -2 to 2
- inner_weight: bfloat16 [768, 3072], P('fsdp'), may hold values from -0.21875 to 0.21875
- inner_bias: bfloat16 [3072], P('fsdp'), may hold values from -2 to 2
- outer_weight: bfloat16 [3072, 768], P('fsdp'), may hold values from -0.109375 to 0.109375
- outer_bias: bfloat16 [768], P('fsdp'), may hold values from -2 to 2
- second_gain: bfloat16 [768], P('fsdp'), may hold values from 0.5 to 1.5
- second_shift: bfloat16 [768], P('fsdp'), may hold values from -2 to 2
Outputs:
- output: bfloat16 [16384, 768], P(('rep', 'fsdp'))
- grad_tokens: bfloat16 [16384, 768], P(('rep', 'fsdp'))
- query_weight_grad: float32 [768, 768], P('fsdp')
- query_bias_grad: float32 [768], P('fsdp')
- key_weight_grad: float32 [768, 768], P('fsdp')
- value_weight_grad: float32 [768, 768], P('fsdp')
- value_bias_grad: float32 [768], P('fsdp')
- out_weight_grad: float32 [768, 768], P('fsdp')
- out_bias_grad: float32 [768], P('fsdp')
- first_gain_grad: float32 [768], P('fsdp')
- first_shift_grad: float32 [768], P('fsdp')
- inner_weight_grad: float32 [768, 3072], P('fsdp')
- inner_bias_grad: float32 [3072], P('fsdp')
- outer_weight_grad: float32 [3072, 768], P('fsdp')
- outer_bias_grad: float32 [768], P('fsdp')
- second_gain_grad: float32 [768], P('fsdp')
- second_shift_grad: float32 [768], P('fsdp')
Inputs may be any that keep to these rules, and one draw needn't show every extreme that they name: Every sequence has at least one token; the longest has exactly 512; the lengths add up to 10240. `slot_seq`: each sequence fills exactly one slot.
All inputs are finite; a program needn't handle non-finite values. No bound on the sum of `lengths` on one device may be relied on, other than what follows from the above.
Results may differ from a plain program's by a relative error of at most 0.017.
Values may be sent and summed in bfloat16 or wider, within the bound.
A program may use at most 128 MiB of HBM per device.

v0:
```python
import functools

import jax
import jax.numpy as jnp
from jax import lax
from jax.experimental import pallas as pl
from jax.experimental.pallas import tpu as pltpu
from jax.sharding import PartitionSpec as P

HEADS = 12
HD = 64
MESH = pl.DeviceIdType.MESH
DMA = pltpu.SemaphoreType.DMA
QUAD = 4
SAVED = 14


norm_eps = 1e-12
masked_score = -1e30
inv_root_two = 0.7071067811865476
inv_root_two_pi = 0.3989422804014327


def remote(src, dst, send, recv, device):
    return pltpu.make_async_remote_copy(
        src_ref=src, dst_ref=dst, send_sem=send, recv_sem=recv,
        device_id=device, device_id_type=MESH,
    )


def place(linear, fsdp_size):
    return {"rep": lax.div(linear, fsdp_size), "fsdp": lax.rem(linear, fsdp_size)}


def enter(count, fsdp_size, me):
    sem = pltpu.get_barrier_semaphore()

    def greet(k, carry):
        pl.semaphore_signal(
            sem, inc=1, device_id=place(lax.rem(me + k, count), fsdp_size), device_id_type=MESH
        )
        return carry

    lax.fori_loop(1, count, greet, 0)
    pl.semaphore_wait(sem, count - 1)


class Exchange:
    def __init__(self, count, fsdp_size, me, src, dst, rows, sems, spread=False):
        self.args = (count, fsdp_size, me, src, dst, rows, sems, spread)

    def copy(self, k, arriving):
        count, fsdp_size, me, src, dst, rows, (send, recv), spread = self.args
        peer = lax.rem(me + k, count)
        slot = lax.rem(me + count - k, count) if arriving else me
        source = src if spread else src.at[pl.ds(pl.multiple_of(peer * rows, rows), rows)]
        return remote(
            source, dst.at[pl.ds(pl.multiple_of(slot * rows, rows), rows)],
            send.at[k], recv.at[k], place(peer, fsdp_size),
        )

    def start(self):
        def go(k, carry):
            self.copy(k, False).start()
            return carry

        lax.fori_loop(1, self.args[0], go, 0)

    def wait(self):
        def go(k, carry):
            self.copy(k, True).wait()
            return carry

        lax.fori_loop(1, self.args[0], go, 0)


def block_of(ref, index, rows):
    return ref.at[pl.ds(pl.multiple_of(index * rows, rows), rows)]


def position(fsdp_size):
    r = lax.axis_index("rep")
    f = lax.axis_index("fsdp")
    core = lax.rem(r, 2)
    chip = lax.div(r, 2)
    q = lax.rem(chip, QUAD)
    return r, f, core, chip, q, chip - q


def flip(q, bit):
    return q + bit - 2 * bit * lax.rem(lax.div(q, bit), 2)


def fetch_kernel(rep_size, fsdp_size, weights, *refs):
    F = fsdp_size
    refs = list(refs)
    take = lambda k: [refs.pop(0) for _ in range(k)]
    slots, tok, cot, length, vec = take(5)
    shard = take(weights)
    otok, ocot, ovec = take(3)
    full = take(weights)
    saved = take(SAVED)
    olen = take(1)[0]
    stage = take(weights)
    held = take(weights)
    x_v, len_v, vec_v, par_v = take(4)
    keep = take(SAVED)
    load_sem, save_sem = take(2)
    (query_v, key_v, value_v, prob_v, context_v, norm1_v, inv1_v, low_v, act_v, slope_v, norm2_v,
     inv2_v, result_v, keptv) = keep
    xs, xr, ys, yr, ls, lr, vs, vr, zs, zr, qs, qr, ps, pr, own = take(15)
    r, f, core, chip, q, base = position(F)
    count = rep_size * F
    me = r * F + f
    rows = tok.shape[0] // count
    vrows = vec.shape[0]
    lrows = length.shape[0]
    enter(count, F, me)

    trade_tok = Exchange(count, F, me, tok, otok, rows, (xs, xr))
    trade_cot = Exchange(count, F, me, cot, ocot, rows, (ys, yr))
    trade_len = Exchange(count, F, me, length, olen, lrows, (ls, lr), spread=True)

    def piece(ref, w, shard_row, quarter):
        S, C = shard[w].shape
        sq, half = S // QUAD, C // 2
        return ref.at[
            pl.ds(pl.multiple_of(shard_row * S + quarter * sq, sq), sq),
            pl.ds(pl.multiple_of(core * half, half), half),
        ]

    def strip(w, shard_row, which):
        S, C = shard[w].shape
        half = C // 2
        return full[w].at[
            pl.ds(pl.multiple_of(shard_row * S, S), S), pl.ds(pl.multiple_of(which * half, half), half)
        ]

    near = (flip(q, 1), flip(q, 2))
    far = flip(near[0], 2)

    def chip_at(quarter):
        return {"rep": (base + quarter) * 2 + core, "fsdp": f}

    partner = {"rep": chip * 2 + (1 - core), "fsdp": f}

    def along(w, row, step):
        source = piece(full[w], w, row, q)
        return remote(
            source, source, zs.at[w, row, (1 - step) // 2], zr.at[w, row], {"rep": r, "fsdp": f + step}
        )

    def first_along(w, step):
        return remote(
            piece(shard[w], w, 0, q), piece(full[w], w, f, q),
            zs.at[w, f, (1 - step) // 2], zr.at[w, f], {"rep": r, "fsdp": f + step},
        )

    def across(w, row, side, arriving):
        part = piece(full[w], w, row, near[side] if arriving else q)
        return remote(part, part, qs.at[w, row, side], qr.at[w, row, side], chip_at(near[side]))

    def relay(w, row, arriving):
        turn = lax.rem(row + w, 2)
        part = piece(full[w], w, row, far if arriving else jnp.where(turn == 0, near[1], near[0]))
        to = chip_at(jnp.where(turn == 0, near[0], near[1]))
        return remote(part, part, qs.at[w, row, 2], qr.at[w, row, 2], to)

    def beside(w, j, arriving):
        row = lax.rem(f + j, F)
        part = strip(w, row, (1 - core) if arriving else core)
        return remote(part, part, ps.at[w, j], pr.at[w, j], partner)

    def vector(j, arriving):
        to = lax.rem(f + j, F)
        row = lax.rem(f + F - j, F) if arriving else f
        return remote(vec, block_of(ovec, row, vrows), vs.at[j], vr.at[j], {"rep": r, "fsdp": to})

    trade_len.start()
    for j in range(1, F):
        vector(j, False).start()
    trade_tok.start()
    for w in range(weights):
        @pl.when(f < F - 1)
        def _():
            first_along(w, 1).start()

        @pl.when(f > 0)
        def _():
            first_along(w, -1).start()

    local = [
        pltpu.make_async_copy(block_of(tok, me, rows), block_of(otok, me, rows), own.at[0]),
        pltpu.make_async_copy(block_of(cot, me, rows), block_of(ocot, me, rows), own.at[1]),
        pltpu.make_async_copy(length, block_of(olen, me, lrows), own.at[2]),
        pltpu.make_async_copy(vec, block_of(ovec, f, vrows), own.at[3]),
    ]
    into = [pltpu.make_async_copy(shard[w], stage[w], own.at[4 + w]) for w in range(weights)]
    for c in local + into:
        c.start()
    out = []
    for w in range(weights):
        into[w].wait()
        c = pltpu.make_async_copy(stage[w], block_of(full[w], f, shard[w].shape[0]), own.at[4 + w])
        c.start()
        out.append(c)

    def step_two(w):
        for d in range(1, F):
            for step in (1, -1):
                row = f - d * step

                @pl.when((row >= 0) & (row < F))
                def _():
                    along(w, row, step).wait_recv()

                    @pl.when((f + step >= 0) & (f + step < F))
                    def _():
                        along(w, row, step).start()

                    across(w, row, 0, False).start()
                    across(w, row, 1, False).start()

    def step_turn(w):
        for j in range(1, F):
            row = lax.rem(f + j, F)
            across(w, row, 0, True).wait_recv()
            across(w, row, 1, True).wait_recv()
            relay(w, row, False).start()

    def step_three(w):
        for j in range(1, F):
            relay(w, lax.rem(f + j, F), True).wait_recv()
            beside(w, j, False).start()

    def step_four(w):
        for j in range(1, F):
            beside(w, j, True).wait_recv()

    steps = (step_two, step_turn, step_three, step_four)

    def advance(at):
        for k, step in enumerate(steps):
            if 0 <= at - k < weights:
                step(at - k)
        done = at - len(steps) + 1
        if 0 <= done < weights:
            out[done].wait()
            pltpu.make_async_copy(full[done], held[done], load_sem.at[done]).start()

    def ready(w):
        pltpu.make_async_copy(full[w], held[w], load_sem.at[w]).wait()

    def store(k):
        pltpu.make_async_copy(keep[k], saved[k], save_sem.at[k]).start()

    n_rows, width = x_v.shape
    f32, bf16 = jnp.float32, jnp.bfloat16

    def project(dst, w, bias):
        tile = 256

        def go(i, carry):
            at = pl.ds(pl.multiple_of(i * tile, tile), tile)
            total = jnp.dot(x_v[...], held[w][:, at], preferred_element_type=f32)
            if bias is not None:
                total = total + par_v[bias : bias + 1, at]
            dst[:, at] = total.astype(bf16)
            return carry

        lax.fori_loop(0, width // tile, go, 0)

    def attend(first, last):
        block = 256
        blocks = n_rows // block

        def go(i, carry):
            pair = lax.div(i, blocks)
            rows_at = pl.ds(pl.multiple_of(lax.rem(i, blocks) * block, block), block)
            lanes = pl.ds(pl.multiple_of(pair * 128, 128), 128)
            lane = lax.broadcasted_iota(jnp.int32, (n_rows, 128), 1)
            queries = query_v[rows_at, lanes]
            keys = key_v[:, lanes]
            values = value_v[:, lanes]
            seen = keptv[0:1, :]
            total = jnp.zeros((block, 128), f32)
            for side in range(2):
                mine = (lane >= side * HD) & (lane < side * HD + HD)
                k_side = jnp.where(mine, keys, jnp.zeros_like(keys))
                v_side = jnp.where(mine, values, jnp.zeros_like(values))
                scores = matmul_right_t(queries, k_side) * HD ** (-0.5)
                scores = jnp.where(seen > 0, scores, masked_score)
                largest = jnp.max(scores, axis=-1, keepdims=True)
                powers = jnp.exp(scores - largest)
                probs = (powers * (1.0 / jnp.sum(powers, axis=-1, keepdims=True))).astype(bf16)
                prob_v[pair * 2 + side, rows_at, :] = probs
                total = total + jnp.dot(probs, v_side, preferred_element_type=f32)
            context_v[rows_at, lanes] = total.astype(bf16)
            return carry

        lax.fori_loop(first * blocks, last * blocks, go, 0)

    def normalize(values):
        center = values - jnp.mean(values, axis=-1, keepdims=True)
        inv = lax.rsqrt(jnp.mean(center * center, axis=-1, keepdims=True) + norm_eps)
        return center * inv, inv

    def first_half():
        block = 128

        def go(i, carry):
            at = pl.ds(pl.multiple_of(i * block, block), block)
            total = jnp.dot(context_v[at, :], held[3][...], preferred_element_type=f32)
            normed, inv = normalize(x_v[at, :].astype(f32) + (total + par_v[2:3, :width]))
            norm1_v[at, :] = normed
            inv1_v[at, :] = jnp.broadcast_to(inv, (block, 128))
            low_v[at, :] = (normed * par_v[3:4, :width] + par_v[4:5, :width]).astype(bf16)
            return carry

        lax.fori_loop(0, n_rows // block, go, 0)

    def widen_out(first, last):
        tile = 256

        def go(i, carry):
            at = pl.ds(pl.multiple_of(i * tile, tile), tile)
            block = 256

            def rows_go(k, c2):
                rows_at = pl.ds(pl.multiple_of(k * block, block), block)
                inner = jnp.dot(low_v[rows_at, :], held[4][:, at], preferred_element_type=f32)
                inner = inner + par_v[8:9, at]
                share = 0.5 * (1.0 + lax.erf(inner * inv_root_two))
                act_v[rows_at, at] = (inner * share).astype(bf16)
                slope = share + inner * jnp.exp(-0.5 * inner * inner) * inv_root_two_pi
                slope_v[rows_at, at] = slope.astype(bf16)
                return c2

            lax.fori_loop(0, n_rows // block, rows_go, 0)
            return carry

        lax.fori_loop(first, last, go, 0)

    def second_half():
        block = 128

        def go(i, carry):
            at = pl.ds(pl.multiple_of(i * block, block), block)
            total = jnp.dot(act_v[at, :], held[5][...], preferred_element_type=f32)
            hidden = norm1_v[at, :] * par_v[3:4, :width] + par_v[4:5, :width]
            normed, inv = normalize(hidden + (total + par_v[5:6, :width]))
            norm2_v[at, :] = normed
            inv2_v[at, :] = jnp.broadcast_to(inv, (block, 128))
            row = lax.broadcasted_iota(jnp.int32, (block, 1), 0) + i * block
            live = row < jnp.max(keptv[1:2, 0:1])
            result = normed * par_v[6:7, :width] + par_v[7:8, :width]
            result_v[at, :] = jnp.where(live, result, 0.0).astype(bf16)
            return carry

        lax.fori_loop(0, n_rows // block, go, 0)
        for k in (10, 11, 12):
            store(k)

    advance(0)
    advance(1)
    advance(2)
    for j in range(1, F):
        vector(j, True).wait()
    trade_len.wait()
    trade_tok.wait()
    for c in local:
        c.wait()
    fill = [
        pltpu.make_async_copy(otok, x_v, load_sem.at[weights]),
        pltpu.make_async_copy(olen, len_v, load_sem.at[weights + 1]),
        pltpu.make_async_copy(ovec, vec_v, load_sem.at[weights + 2]),
    ]
    for c in fill:
        c.start()
    for c in fill:
        c.wait()
    narrow = jnp.zeros((8, width), f32)
    for k in range(F):
        narrow = narrow + vec_v[k * vrows : k * vrows + 16, :].astype(f32)[0:8, :]
    par_v[0:8, 0:width] = narrow
    part = shard[5].shape[0]
    for k in range(F):
        par_v[8:9, k * part : (k + 1) * part] = vec_v[k * vrows : k * vrows + 16, :].astype(f32)[8:9, 0:part]
    mine = slots[me]
    owner = lax.div(lax.broadcasted_iota(jnp.int32, len_v.shape, 0), lrows)
    my_length = jnp.max(jnp.where(owner == mine, len_v[...], 0))
    key_at = lax.broadcasted_iota(jnp.int32, (8, n_rows), 1)
    second = lax.broadcasted_iota(jnp.int32, (8, n_rows), 0) > 0
    keptv[...] = jnp.where(second, my_length, (key_at < my_length).astype(jnp.int32))
    advance(3)
    ready(0)
    project(query_v, 0, 0)
    advance(4)
    ready(1)
    project(key_v, 1, None)
    advance(5)
    trade_cot.start()
    ready(2)
    project(value_v, 2, 1)
    for k in (0, 1, 2):
        store(k)
    attend(0, 2)
    advance(6)
    attend(2, 4)
    advance(7)
    attend(4, 6)
    for k in (3, 4):
        store(k)
    ready(3)
    first_half()
    for k in (5, 6, 7):
        store(k)
    tiles = held[4].shape[1] // 256
    ready(4)
    widen_out(0, tiles // 2)
    advance(8)
    widen_out(tiles // 2, tiles)
    for k in (8, 9):
        store(k)
    ready(5)
    second_half()
    store(13)
    for w in range(weights):
        for step in (1, -1):

            @pl.when((f + step >= 0) & (f + step < F))
            def _():
                first_along(w, step).wait_send()
                for d in range(1, F):
                    row = f - d * step

                    @pl.when((row >= 0) & (row < F))
                    def _():
                        along(w, row, step).wait_send()

        for j in range(1, F):
            row = lax.rem(f + j, F)
            across(w, row, 0, False).wait_send()
            across(w, row, 1, False).wait_send()
            relay(w, row, False).wait_send()
            beside(w, j, False).wait_send()
    trade_cot.wait()
    for k in range(SAVED):
        pltpu.make_async_copy(keep[k], saved[k], save_sem.at[k]).wait()


def fetch(rep_size, fsdp_size, slots, tok, cot, length, vec, shards_in):
    weights = len(shards_in)
    count = rep_size * fsdp_size
    F = fsdp_size
    like = jax.ShapeDtypeStruct
    n_rows, width = tok.shape
    hidden_width = shards_in[4].shape[1]
    bf16, f32 = jnp.bfloat16, jnp.float32
    rows_of = lambda columns, kind: like((n_rows, columns), kind)
    save = [rows_of(width, bf16)] * 3 + [like((HEADS, n_rows, n_rows), bf16), rows_of(width, bf16)]
    save += [rows_of(width, f32), rows_of(128, f32), rows_of(width, bf16)]
    save += [rows_of(hidden_width, bf16)] * 2 + [rows_of(width, f32), rows_of(128, f32), rows_of(width, bf16)]
    save += [like((8, n_rows), jnp.int32)]
    wide = [like((w.shape[0] * F, w.shape[1]), w.dtype) for w in shards_in]
    outs = [
        like(tok.shape, tok.dtype), like(cot.shape, cot.dtype),
        like((F * vec.shape[0], vec.shape[1]), vec.dtype),
    ] + wide + save + [like((count * length.shape[0], length.shape[1]), length.dtype)]
    anywhere = pl.BlockSpec(memory_space=pl.ANY)
    V = lambda a: pltpu.VMEM(a.shape, a.dtype)
    return pl.pallas_call(
        functools.partial(fetch_kernel, rep_size, fsdp_size, weights),
        out_shape=outs,
        in_specs=[pl.BlockSpec(memory_space=pltpu.SMEM)] + [anywhere] * (4 + weights),
        out_specs=[anywhere] * len(outs),
        scratch_shapes=[V(w) for w in shards_in]
        + [V(w) for w in wide]
        + [V(tok), V(outs[-1]), V(outs[2]), pltpu.VMEM((16, hidden_width), f32)]
        + [V(a) for a in save]
        + [DMA((weights + 3,)), DMA((SAVED,))]
        + [DMA((count,))] * 6
        + [DMA((F,))] * 2
        + [DMA((weights, F, 2)), DMA((weights, F))]
        + [DMA((weights, F, 3))] * 2
        + [DMA((weights, F))] * 2
        + [DMA((4 + weights,))],
        compiler_params=pltpu.CompilerParams(
            collective_id=1, has_side_effects=True, vmem_limit_bytes=60 * 2**20
        ),
        name="forward",
    )(slots, tok, cot, length, vec, *shards_in)


def add_into(dst, left, parts, rows):
    def go(i, carry):
        at = pl.ds(pl.multiple_of(i * rows, rows), rows)
        total = left[at, :].astype(jnp.float32)
        for part in parts:
            total = total + part[at, :].astype(jnp.float32)
        dst[at, :] = total.astype(dst.dtype)
        return carry

    lax.fori_loop(0, dst.shape[0] // rows, go, 0)


def reduce_kernel(rep_size, fsdp_size, weights, *refs):
    F = fsdp_size
    refs = list(refs)
    take = lambda k: [refs.pop(0) for _ in range(k)]
    res, gin = take(2)
    grads = take(weights)
    ores, ogin = take(2)
    owned = take(weights)
    half_in = take(weights)
    half_own = take(weights)
    quad_in = take(weights)
    quad_sum = take(weights)
    line_in = take(weights)
    line_sum = take(weights)
    group_count = rep_size // (2 * QUAD)
    group_in = take(weights) if group_count > 1 else None
    xs, xr, ys, yr, ps, pr, qs, qr, zs, zr, gs, gr, hs, hr, bs, br, own = take(17)
    r, f, core, chip, q, base = position(F)
    count = rep_size * F
    me = r * F + f
    rows = res.shape[0] // count
    enter(count, F, me)

    trade_res = Exchange(count, F, me, res, ores, rows, (xs, xr))
    trade_gin = Exchange(count, F, me, gin, ogin, rows, (ys, yr))
    partner = {"rep": chip * 2 + (1 - core), "fsdp": f}

    def mate(m):
        return {"rep": (base + lax.rem(q + m, QUAD)) * 2 + core, "fsdp": f}

    def columns(ref, w, which):
        half = grads[w].shape[1] // 2
        return ref.at[:, pl.ds(pl.multiple_of(which * half, half), half)]

    def swap(w):
        return remote(columns(grads[w], w, 1 - core), half_in[w], ps.at[w], pr.at[w], partner)

    def size(w):
        S = grads[w].shape[0] // F
        return S, S // QUAD

    near = (flip(q, 1), flip(q, 2))
    far = flip(near[0], 2)

    def chip_at(quarter):
        return {"rep": (base + quarter) * 2 + core, "fsdp": f}

    def rows_of(w, t, quarter):
        S, sq = size(w)
        return pl.ds(pl.multiple_of(t * S + quarter * sq, sq), sq)

    def across(w, t, k):
        side = (w + t) % 2
        return remote(
            half_in[w].at[rows_of(w, t, (near[side], far)[k])], quad_in[w].at[k, t],
            qs.at[w, t, k], qr.at[w, t, k], chip_at(near[side]),
        )

    def turn(w, t):
        side = 1 - (w + t) % 2
        return remote(
            half_in[w].at[rows_of(w, t, near[side])], quad_in[w].at[2, t],
            qs.at[w, t, 2], qr.at[w, t, 2], chip_at(near[side]),
        )

    def along(w, j):
        S, sq = size(w)
        to = lax.rem(f + j, F)
        return remote(
            quad_sum[w].at[pl.ds(pl.multiple_of(to * sq, sq), sq)], line_in[w].at[j - 1],
            zs.at[w, j], zr.at[w, j], {"rep": r, "fsdp": to},
        )

    def group(w, g):
        to = lax.rem(lax.div(chip, QUAD) + g, group_count)
        return remote(
            line_sum[w], group_in[w].at[g - 1], gs.at[w, g], gr.at[w, g],
            {"rep": (to * QUAD + q) * 2 + core, "fsdp": f},
        )

    def home(w, quarter, which):
        S, sq = size(w)
        half = grads[w].shape[1] // 2
        return owned[w].at[
            pl.ds(pl.multiple_of(quarter * sq, sq), sq), pl.ds(pl.multiple_of(which * half, half), half)
        ]

    def spread(w, m, arriving):
        S, sq = size(w)
        return remote(
            line_sum[w], home(w, lax.rem(q + QUAD - m, QUAD) if arriving else q, core),
            hs.at[w, m], hr.at[w, m], mate(m),
        )

    def beside(w, arriving):
        part = columns(owned[w], w, (1 - core) if arriving else core)
        return remote(part, part, bs.at[w], br.at[w], partner)

    for w in range(weights):
        swap(w).start()
    local = [
        pltpu.make_async_copy(block_of(res, me, rows), block_of(ores, me, rows), own.at[0]),
        pltpu.make_async_copy(block_of(gin, me, rows), block_of(ogin, me, rows), own.at[1]),
    ]
    kept = [
        pltpu.make_async_copy(columns(grads[w], w, core), half_own[w], own.at[2 + w])
        for w in range(weights)
    ]
    for c in local + kept:
        c.start()

    def step_one(w):
        kept[w].wait()
        swap(w).wait_recv()
        add_into(half_in[w], half_in[w], [half_own[w]], size(w)[1])
        for t in range(F):
            for k in range(2):
                across(w, t, k).start()

    def step_turn(w):
        for t in range(F):
            for k in range(2):
                across(w, t, k).wait_recv()
            at = rows_of(w, t, near[1 - (w + t) % 2])
            total = half_in[w][at, :].astype(jnp.float32) + quad_in[w][1, t].astype(jnp.float32)
            half_in[w][at, :] = total.astype(half_in[w].dtype)
            turn(w, t).start()

    def step_two(w):
        S, sq = size(w)
        for t in range(F):
            turn(w, t).wait_recv()
            total = half_in[w][rows_of(w, t, q), :].astype(jnp.float32)
            total = total + quad_in[w][0, t].astype(jnp.float32) + quad_in[w][2, t].astype(jnp.float32)
            quad_sum[w][pl.ds(t * sq, sq), :] = total.astype(quad_sum[w].dtype)
        for j in range(1, F):
            along(w, j).start()

    def step_three(w):
        S, sq = size(w)
        for j in range(1, F):
            along(w, j).wait_recv()
        total = quad_sum[w][pl.ds(pl.multiple_of(f * sq, sq), sq), :].astype(jnp.float32)
        for j in range(F - 1):
            total = total + line_in[w][j].astype(jnp.float32)
        line_sum[w][...] = total.astype(line_sum[w].dtype)
        for g in range(1, group_count):
            group(w, g).start()
        if group_count == 1:
            finish(w)

    def step_group(w):
        for g in range(1, group_count):
            group(w, g).wait()
        total = line_sum[w][...].astype(jnp.float32)
        for g in range(group_count - 1):
            total = total + group_in[w][g].astype(jnp.float32)
        line_sum[w][...] = total.astype(line_sum[w].dtype)
        finish(w)

    def finish(w):
        for m in range(1, QUAD):
            spread(w, m, False).start()
        c = pltpu.make_async_copy(line_sum[w], home(w, q, core), own.at[2 + w])
        c.start()
        c.wait()

    def step_four(w):
        for m in range(1, QUAD):
            spread(w, m, True).wait_recv()
        beside(w, False).start()

    steps = [step_one, step_turn, step_two, step_three] + ([step_group] if group_count > 1 else []) + [step_four]
    for at in range(weights + len(steps) - 1):
        for k, step in enumerate(steps):
            if 0 <= at - k < weights:
                step(at - k)
        if at == 0:
            trade_res.start()
            trade_gin.start()
    for w in range(weights):
        beside(w, True).wait_recv()
        swap(w).wait_send()
        for t in range(F):
            across(w, t, 0).wait_send()
            across(w, t, 1).wait_send()
            turn(w, t).wait_send()
        for m in range(1, QUAD):
            spread(w, m, False).wait_send()
        for j in range(1, F):
            along(w, j).wait_send()
        beside(w, False).wait_send()
    for c in local:
        c.wait()
    trade_res.wait()
    trade_gin.wait()


def reduce_all(rep_size, fsdp_size, res, gin, grads):
    weights = len(grads)
    count = rep_size * fsdp_size
    F = fsdp_size
    groups = rep_size // (2 * QUAD)
    like = jax.ShapeDtypeStruct
    anywhere = pl.BlockSpec(memory_space=pl.ANY)
    outs = [like(res.shape, res.dtype), like(gin.shape, gin.dtype)] + [
        like((g.shape[0] // F, g.shape[1]), g.dtype) for g in grads
    ]
    V = pltpu.VMEM
    scratch = [V((g.shape[0], g.shape[1] // 2), g.dtype) for g in grads]
    scratch += [V((g.shape[0], g.shape[1] // 2), g.dtype) for g in grads]
    scratch += [V((3, F, g.shape[0] // QUAD // F, g.shape[1] // 2), g.dtype) for g in grads]
    scratch += [V((g.shape[0] // QUAD, g.shape[1] // 2), g.dtype) for g in grads]
    scratch += [V((F - 1, g.shape[0] // QUAD // F, g.shape[1] // 2), g.dtype) for g in grads]
    scratch += [V((g.shape[0] // QUAD // F, g.shape[1] // 2), g.dtype) for g in grads]
    if groups > 1:
        scratch += [V((groups - 1, g.shape[0] // QUAD // F, g.shape[1] // 2), g.dtype) for g in grads]
    scratch += [DMA((count,))] * 4 + [DMA((weights,))] * 2 + [DMA((weights, F, 3))] * 2
    scratch += [DMA((weights, F))] * 2 + [DMA((weights, max(groups, 2)))] * 2
    scratch += [DMA((weights, QUAD))] * 2 + [DMA((weights,))] * 2 + [DMA((2 + weights,))]
    return pl.pallas_call(
        functools.partial(reduce_kernel, rep_size, fsdp_size, weights),
        out_shape=outs,
        in_specs=[anywhere] * (2 + weights),
        out_specs=[anywhere] * (2 + weights),
        scratch_shapes=scratch,
        compiler_params=pltpu.CompilerParams(
            collective_id=2, has_side_effects=True, vmem_limit_bytes=56 * 2**20
        ),
        name="reduce_all",
    )(res, gin, *grads)


def widen_kernel(count, *refs):
    for k in range(count):
        refs[count + k][...] = refs[k][...].astype(jnp.float32)


def widen(arrays):
    steps = 4

    def spec(a):
        return pl.BlockSpec((a.shape[0] // steps, a.shape[1]), lambda i: (i, 0))

    return pl.pallas_call(
        functools.partial(widen_kernel, len(arrays)),
        grid=(steps,),
        in_specs=[spec(a) for a in arrays],
        out_specs=[spec(a) for a in arrays],
        out_shape=[jax.ShapeDtypeStruct(a.shape, jnp.float32) for a in arrays],
        name="widen",
    )(*arrays)


def matmul(left, right):
    return jnp.dot(left, right, preferred_element_type=jnp.float32)


def matmul_left_t(left, right):
    return lax.dot_general(
        left, right, (((0,), (0,)), ((), ())), preferred_element_type=jnp.float32
    )


def matmul_right_t(left, right):
    return lax.dot_general(
        left, right, (((1,), (1,)), ((), ())), preferred_element_type=jnp.float32
    )


def norm_backward(grad_out, normed, scaled_inv, norm_gain):
    grad_normed = grad_out * norm_gain
    first_mean = jnp.mean(grad_normed, axis=-1, keepdims=True)
    second_mean = jnp.mean(grad_normed * normed, axis=-1, keepdims=True)
    return (grad_normed - first_mean - normed * second_mean) * scaled_inv


def shards(
    tokens,
    cotangent,
    lengths,
    slot_seq,
    query_weight,
    query_bias,
    key_weight,
    value_weight,
    value_bias,
    out_weight,
    out_bias,
    first_gain,
    first_shift,
    inner_weight,
    inner_bias,
    outer_weight,
    outer_bias,
    second_gain,
    second_shift,
):
    rep_size, fsdp_size = lax.axis_size("rep"), lax.axis_size("fsdp")
    me = lax.axis_index("rep") * fsdp_size + lax.axis_index("fsdp")
    row_count, feature_dim = tokens.shape
    small = [query_bias, value_bias, out_bias, first_gain, first_shift, outer_bias, second_gain, second_shift]
    width = query_bias.shape[0]
    wide = inner_bias.shape[0] // width
    lanes = 256
    vec_rows = 16
    chosen = jnp.arange(fsdp_size, dtype=jnp.int32) == lax.axis_index("fsdp")

    def own_lanes(v):
        return jnp.where(chosen[:, None], v[None, :], jnp.zeros_like(v)[None, :]).reshape(-1)

    last = jnp.pad(inner_bias, (0, max(0, feature_dim - inner_bias.shape[0])))
    vec = jnp.pad(jnp.stack([own_lanes(v) for v in small] + [last]), ((0, vec_rows - 9), (0, 0)))
    length_block = jnp.broadcast_to(lengths.reshape(1, 1), (8, 128))
    (
        seq_rows, seq_seed, all_vec,
        query_full, key_full, value_full, out_full, inner_full, outer_full,
        query_rows, key_rows, value_rows, probs, context, first_normed, first_inv, hidden_low,
        activated, slope, second_normed, second_inv, result, kept_table, _,
    ) = fetch(
        rep_size, fsdp_size, slot_seq, tokens, cotangent, length_block, vec,
        [query_weight, key_weight, value_weight, out_weight, inner_weight, outer_weight],
    )
    kept = kept_table[0] > 0
    params = all_vec.reshape(fsdp_size, vec_rows, feature_dim)[:, :8].astype(jnp.float32).sum(axis=0)
    first_gain_full, second_gain_full = params[3], params[6]
    first_inv, second_inv = first_inv[:, :1], second_inv[:, :1]
    head_shape = (row_count, HEADS, HD)
    seed_rows = jnp.where(kept[:, None], seq_seed.astype(jnp.float32), 0.0)
    grad_second_gain = jnp.sum(seed_rows * second_normed, axis=0)
    grad_second_shift = jnp.sum(seed_rows, axis=0)
    grad_second = norm_backward(seed_rows, second_normed, second_inv, second_gain_full)
    grad_outer = grad_second.astype(jnp.bfloat16)
    grad_outer_bias = jnp.sum(grad_outer, axis=0, dtype=jnp.float32)
    grad_outer_weight = matmul_left_t(activated, grad_outer)
    grad_activated = matmul_right_t(grad_outer, outer_full)
    grad_inner = (grad_activated * slope).astype(jnp.bfloat16)
    grad_inner_bias = jnp.sum(grad_inner, axis=0, dtype=jnp.float32)
    grad_inner_weight = matmul_left_t(hidden_low, grad_inner)
    grad_hidden = grad_second + matmul_right_t(grad_inner, inner_full)
    grad_first_gain = jnp.sum(grad_hidden * first_normed, axis=0)
    grad_first_shift = jnp.sum(grad_hidden, axis=0)
    grad_residual = norm_backward(grad_hidden, first_normed, first_inv, first_gain_full)
    grad_attended = grad_residual.astype(jnp.bfloat16)
    grad_out_bias = jnp.sum(grad_attended, axis=0, dtype=jnp.float32)
    grad_out_weight = matmul_left_t(context, grad_attended)
    grad_context = matmul_right_t(grad_attended, out_full).astype(jnp.bfloat16)
    heads_of = lambda a: a.reshape(head_shape)
    grad_rows_h = heads_of(grad_context)
    prob32 = probs.astype(jnp.float32)
    grad_prob = jnp.einsum(
        "qhd,khd->hqk", grad_rows_h, heads_of(value_rows), preferred_element_type=jnp.float32
    )
    centered = jnp.sum(prob32 * grad_prob, axis=-1, keepdims=True)
    grad_scores = (prob32 * (grad_prob - centered)).astype(jnp.bfloat16)
    back = lambda eq, a, b, scale: (
        (jnp.einsum(eq, a, b, preferred_element_type=jnp.float32) * scale)
        .astype(jnp.bfloat16).reshape(row_count, feature_dim)
    )
    scale = HD ** (-0.5)
    grad_query = back("hqk,khd->qhd", grad_scores, heads_of(key_rows), scale)
    grad_key = back("hqk,qhd->khd", grad_scores, heads_of(query_rows), scale)
    grad_value = back("hqk,qhd->khd", probs, grad_rows_h, 1.0)
    grad_query_bias = jnp.sum(grad_query, axis=0, dtype=jnp.float32)
    grad_value_bias = jnp.sum(grad_value, axis=0, dtype=jnp.float32)
    grad_query_weight = matmul_left_t(seq_rows, grad_query)
    grad_key_weight = matmul_left_t(seq_rows, grad_key)
    grad_value_weight = matmul_left_t(seq_rows, grad_value)
    grad_input = (
        grad_residual
        + matmul_right_t(grad_query, query_full)
        + matmul_right_t(grad_key, key_full)
        + matmul_right_t(grad_value, value_full)
    ).astype(jnp.bfloat16)
    low = lambda g: g.astype(jnp.bfloat16)
    grad_small = [
        grad_query_bias, grad_value_bias, grad_out_bias, grad_first_gain, grad_first_shift,
        grad_outer_bias, grad_second_gain, grad_second_shift,
    ]
    grad_table = jnp.concatenate(
        [
            jnp.stack(grad_small).reshape(8, fsdp_size, width).transpose(1, 0, 2),
            grad_inner_bias.reshape(fsdp_size, wide, width),
        ],
        axis=1,
    )
    grad_rows = 32
    grad_table = jnp.pad(
        grad_table, ((0, 0), (0, grad_rows - 8 - wide), (0, lanes - width))
    ).reshape(fsdp_size * grad_rows, lanes)
    (
        back_rows, back_grads, d_outer, d_inner, d_out, d_query, d_key, d_value, d_vec,
    ) = reduce_all(
        rep_size, fsdp_size, result, grad_input,
        [
            low(grad_outer_weight), low(grad_inner_weight), low(grad_out_weight),
            low(grad_query_weight), low(grad_key_weight), low(grad_value_weight), grad_table,
        ],
    )
    d_outer, d_inner, d_out, d_query, d_key, d_value = widen(
        [d_outer, d_inner, d_out, d_query, d_key, d_value]
    )
    v = d_vec[:, :width]
    return (
        back_rows, back_grads,
        d_query, v[0], d_key, d_value, v[1], d_out, v[2], v[3], v[4],
        d_inner, v[8 : 8 + wide].reshape(-1), d_outer, v[5], v[6], v[7],
    )


def solution(mesh):
    placed = (
        P(("rep", "fsdp"), None),
        P(("rep", "fsdp"), None),
        P(("rep", "fsdp")),
        P(),
        P("fsdp", None),
        P("fsdp"),
        P("fsdp", None),
        P("fsdp", None),
        P("fsdp"),
        P("fsdp", None),
        P("fsdp"),
        P("fsdp"),
        P("fsdp"),
        P("fsdp", None),
        P("fsdp"),
        P("fsdp", None),
        P("fsdp"),
        P("fsdp"),
        P("fsdp"),
    )
    return jax.shard_map(
        shards,
        mesh=mesh,
        in_specs=placed,
        out_specs=(
            P(("rep", "fsdp"), None),
            P(("rep", "fsdp"), None),
            P("fsdp", None),
            P("fsdp"),
            P("fsdp", None),
            P("fsdp", None),
            P("fsdp"),
            P("fsdp", None),
            P("fsdp"),
            P("fsdp"),
            P("fsdp"),
            P("fsdp", None),
            P("fsdp"),
            P("fsdp", None),
            P("fsdp"),
            P("fsdp"),
            P("fsdp"),
        ),
        check_vma=False,
    )
```

profile of v0, /device:TPU:0, one launch (start us, length us, event | category | flops | bytes accessed | tf_op | source)
XLA Modules:
  0.0 321.7 jit_solution(9512168352207094445)
XLA Ops:
  1.9 0.8 broadcast_select_fusion
  4.8 123.7 %forward.1 = (bf16[512,768]{1,0:T(8,128)(2,1)}, bf16[512,768]{1,0:T(8,128)(2,1)}, bf16[64,768]{1,0:T(8,128)(2,1)}, bf16[768,768]{1,0:T(8,128)(2,1)}, bf16[768,76...) custom-call(s32[32]{0:T(128)} %refs_0_.1, ...), custom_call_target="tpu_custom_call" | custom-call | tf_op jit(solution)/shard_map/forward/pallas_call | solution.py:472
  128.5 1.5 copy.48
  130.1 1.3 slice_reduce_fusion
  132.2 2.0 multiply_reduce_fusion
  134.8 5.4 %convert_reduce_fusion = (f32[3072]{0:T(1024)S(1)}, bf16[512,3072]{1,0:T(8,128)(2,1)S(1)}) fusion(bf16[512,3072]{1,0:T(8,128)(2,1)} %get-tuple-element.62, bf16[3072,768]{1,0:T(8,128)(2,1)S(1)} %copy-done.16, f32[512,768]{1,0:T(8,128)S(1)} %get-tuple-element.104), kind=kOutput, calls=%fused_computation.4 | convolution fusion | flops 2424173568 | bytes 12595200 | tf_op jit(solution)/shard_map/dot_general | solution.py:772
  140.2 3.0 multiply_reduce_fusion.1
  143.7 1.1 copy-done.1
  144.8 0.8 convolution_convert_fusion.6
  145.9 1.4 copy.45
  147.4 5.1 %fusion = (f32[12,512]{1,0:T(8,128)S(1)}, f32[12,512,512]{2,1,0:T(8,128)S(1)}) fusion(bf16[12,512,512]{2,1,0:T(8,128)(2,1)} %get-tuple-element.67, bf16[512,12,64]{0,2,1:T(8,128)(2,1)S(1)} %bitcast.60, bf16[512,12,64]{0,2,1:T(8,128)(2,1)S(1)} %bitcast.65), kind=kOutput, calls=%fused_computation.2 | convolution fusion | flops 412084224 | bytes 20471808 | tf_op jit(solution)/shard_map/qhd,khd->hqk/dot_general | solution.py:857
  152.5 1.7 fusion.1
  154.2 1.1 multiply_convert_fusion.1
  155.4 1.5 copy-done
  156.9 2.0 fusion.11
  158.8 2.4 copy.43
  161.3 5.3 %convert_reduce_fusion.4 = (f32[12,64]{1,0:T(8,128)S(1)}, bf16[12,64,512]{2,1,0:T(8,128)(2,1)S(1)}) fusion(bf16[512,12,64]{0,2,1:T(8,128)(2,1)} %bitcast.66, bf16[12,512,512]{2,1,0:T(8,128)(2,1)} %copy-done), kind=kOutput, calls=%fused_computation.13 | convolution fusion | flops 404225280 | bytes 7867392 | tf_op jit(solution)/shard_map/hqk,khd->qhd/dot_general | solution.py:863
  166.5 0.8 fusion.10
  167.4 1.1 convert_reduce_fusion.3
  169.6 1.8 add_convert_fusion.refs_1_
  171.4 0.8 copy-done.17
  172.3 4.3 %convolution_convert_fusion.1.refs_2_ = bf16[3072,768]{1,0:T(8,128)(2,1)} fusion(bf16[512,3072]{1,0:T(8,128)(2,1)S(1)} %copy-done.17, f32[512,768]{1,0:T(8,128)S(1)} %copy-done.10), kind=kOutput, calls=%fused_computation.7 | convolution fusion | flops 2418671616 | bytes 9437184 | tf_op jit(solution)/shard_map/dot_general | solution.py:766
  176.6 4.4 %convolution_convert_fusion.refs_3_ = bf16[768,3072]{1,0:T(8,128)(2,1)} fusion(bf16[512,768]{1,0:T(8,128)(2,1)S(1)} %copy-done.22, bf16[512,3072]{1,0:T(8,128)(2,1)S(1)} %copy-done.24), kind=kOutput, calls=%fused_computation.6 | convolution fusion | flops 2418278400 | bytes 8650752 | tf_op jit(solution)/shard_map/dot_general | solution.py:766
  181.0 1.8 convolution_convert_fusion.5.refs_4_
  182.9 1.8 convolution_convert_fusion.4.refs_5_
  184.7 1.8 convolution_convert_fusion.3.refs_6_
  186.5 1.9 convolution_convert_fusion.2.refs_7_
  189.8 121.8 %reduce_all.1 = (bf16[512,768]{1,0:T(8,128)(2,1)}, bf16[512,768]{1,0:T(8,128)(2,1)}, bf16[768,768]{1,0:T(8,128)(2,1)}, bf16[192,3072]{1,0:T(8,128)(2,1)}, bf16[1...) custom-call(bf16[512,768]{1,0:T(8,128)(2,1)} %get-tuple-element.55.r, ...), custom_call_target="tpu_custom_call" | custom-call | tf_op jit(solution)/shard_map/reduce_all/pallas_call | solution.py:727
  311.6 5.3 %widen.1 = (f32[768,768]{1,0:T(8,128)}, f32[192,3072]{1,0:T(8,128)}, f32[192,768]{1,0:T(8,128)}, f32[192,768]{1,0:T(8,128)}, f32[192,768]{1,0:T(8,128)}, /*index=5*/f32[192,768]{1,0:T(8,128)}) custom-call(bf16[768,768]{1,0:T(8,128)(2,1)} %get-tuple-element.80.refs_0_, bf16[192,3072]{1,0:T(8,128)(2,1)} %get-tuple-element.81.refs_1_, ...), custom_call_target="tpu_custom_call" | custom-call | tf_op jit(solution)/shard_map/widen/pallas_call | solution.py:751
  316.9 1.6 fusion.9
  319.9 0.9 copy.53
  320.8 0.9 copy.54
  (97 shorter events, 8.6 us)
Async XLA Ops:
  128.5 2.9 copy-start.15
  128.5 3.7 %copy-start.3 = (f32[512,768]{1,0:T(8,128)S(1)}, f32[512,768]{1,0:T(8,128)}, u32[]{:S(2)}) copy-start(f32[512,768]{1,0:T(8,128)} %get-tuple-element.59) | copy-start | bytes 4718596
  130.1 4.1 %copy-start.4 = (bf16[512,768]{1,0:T(8,128)(2,1)S(1)}, bf16[512,768]{1,0:T(8,128)(2,1)}, u32[]{:S(2)}) copy-start(bf16[512,768]{1,0:T(8,128)(2,1)} %get-tuple-element.57) | copy-start | bytes 2359300
  132.2 2.6 copy-start.16
  134.2 6.0 %slice-start.4 = ((s8[4718592]{0:T(1024)(128)(4,1)}), s8[4194304]{0:T(1024)(128)(4,1)S(1)}, s32[]{:S(2)}) async-start(s8[4718592]{0:T(1024)(128)(4,1)} %bitcast.82), calls=%async_computation.4 | async-start | bytes 8388608
  134.7 5.4 %copy-start.9 = (f32[512,768]{1,0:T(8,128)}, f32[512,768]{1,0:T(8,128)S(1)}, u32[]{:S(2)}) copy-start(f32[512,768]{1,0:T(8,128)S(1)} %get-tuple-element.104) | copy-start | bytes 4718596
  134.8 5.4 %copy-start.7 = (f32[512,768]{1,0:T(8,128)S(1)}, f32[512,768]{1,0:T(8,128)}, u32[]{:S(2)}) copy-start(f32[512,768]{1,0:T(8,128)} %get-tuple-element.64) | copy-start | bytes 4718596
  134.8 5.4 %slice-start.5 = ((s8[4718592]{0:T(1024)(128)(4,1)}), s8[524288]{0:T(1024)(128)(4,1)S(1)}, s32[]{:S(2)}) async-start(s8[4718592]{0:T(1024)(128)(4,1)} %bitcast.82), calls=%async_computation.5 | async-start | bytes 1048576
  140.1 3.1 copy-start.23
  143.2 1.6 copy-start.20
  143.6 1.1 copy-start.1
  147.3 5.1 %slice-start = ((s8[6291456]{0:T(1024)(128)(4,1)}), s8[4194304]{0:T(1024)(128)(4,1)S(1)}, s32[]{:S(2)}) async-start(s8[6291456]{0:T(1024)(128)(4,1)} %bitcast.56), calls=%async_computation | async-start | bytes 8388608
  147.3 5.1 %slice-start.1 = ((s8[6291456]{0:T(1024)(128)(4,1)}), s8[2097152]{0:T(1024)(128)(4,1)S(1)}, s32[]{:S(2)}) async-start(s8[6291456]{0:T(1024)(128)(4,1)} %bitcast.56), calls=%async_computation.1 | async-start | bytes 4194304
  154.2 2.7 copy-start
  154.2 2.7 copy-start.19
  156.9 2.0 copy-start.5
  158.8 8.5 %slice-start.2 = ((s8[6291456]{0:T(1024)(128)(4,1)}), s8[2097152]{0:T(1024)(128)(4,1)S(1)}, s32[]{:S(2)}) async-start(s8[6291456]{0:T(1024)(128)(4,1)} %bitcast.58), calls=%async_computation.2 | async-start | bytes 4194304
  161.3 5.3 %copy-start.18 = (bf16[768,768]{1,0:T(8,128)(2,1)S(1)}, bf16[768,768]{1,0:T(8,128)(2,1)}, u32[]{:S(2)}) copy-start(bf16[768,768]{1,0:T(8,128)(2,1)} %get-tuple-element.70) | copy-start | bytes 3538948
  161.3 6.1 %slice-start.3 = ((s8[6291456]{0:T(1024)(128)(4,1)}), s8[4194304]{0:T(1024)(128)(4,1)S(1)}, s32[]{:S(2)}) async-start(s8[6291456]{0:T(1024)(128)(4,1)} %bitcast.58), calls=%async_computation.3 | async-start | bytes 8388608
  167.4 1.4 copy-start.2
  167.4 1.9 copy-start.8
  167.4 2.2 copy-start.11
  169.6 1.8 copy-start.10
  169.6 2.6 copy-start.17
  172.3 4.3 %copy-start.22 = (bf16[512,768]{1,0:T(8,128)(2,1)S(1)}, bf16[512,768]{1,0:T(8,128)(2,1)}, u32[]{:S(2)}) copy-start(bf16[512,768]{1,0:T(8,128)(2,1)} %get-tuple-element.75) | copy-start | bytes 2359300
  172.3 4.3 %copy-start.24 = (bf16[512,3072]{1,0:T(8,128)(2,1)S(1)}, bf16[512,3072]{1,0:T(8,128)(2,1)}, u32[]{:S(2)}) copy-start(bf16[512,3072]{1,0:T(8,128)(2,1)} %copy-done.23) | copy-start | bytes 9437188
  176.6 4.4 %copy-start.12 = (bf16[512,768]{1,0:T(8,128)(2,1)S(1)}, bf16[512,768]{1,0:T(8,128)(2,1)}, u32[]{:S(2)}) copy-start(bf16[512,768]{1,0:T(8,128)(2,1)} %get-tuple-element.76) | copy-start | bytes 2359300
  181.0 1.8 copy-start.21
  182.9 1.8 copy-start.6
  311.6 8.3 %copy-start.14 = (bf16[512,768]{1,0:T(8,128)(2,1)S(1)}, bf16[512,768]{1,0:T(8,128)(2,1)}, u32[]{:S(2)}) copy-start(bf16[512,768]{1,0:T(8,128)(2,1)} %get-tuple-element.153) | copy-start | bytes 2359300
  316.9 3.8 %copy-start.13 = (bf16[512,768]{1,0:T(8,128)(2,1)S(1)}, bf16[512,768]{1,0:T(8,128)(2,1)}, u32[]{:S(2)}) copy-start(bf16[512,768]{1,0:T(8,128)(2,1)} %get-tuple-element.154) | copy-start | bytes 2359300
where the time goes:
time: 322 us
  Pallas kernels  251 us (78%)
  matrix products  42.5 us (13%)
  local copies, waits for them, and re-layouts  19.8 us (6%)
  other arithmetic  6.9 us (2%)
    pallas_call x1, Pallas kernels, fetch(): pl.pallas_call(functools.partial(fetch_kernel, rep_size, fsdp_size, weigh...  124 us
    pallas_call x1, Pallas kernels, reduce_all(): pl.pallas_call(functools.partial(reduce_kernel, rep_size, fsdp_size, weig...  122 us
    dot_general x6, matrix products, matmul_left_t(): lax.dot_general(left, right, (((0,), (0,)), ((), ())), preferred_element_...  16.1 us
    dot_general x6, matrix products, matmul_right_t(): lax.dot_general(left, right, (((1,), (1,)), ((), ())), preferred_element_...  13.8 us
    dot_general x3, matrix products, shards(): jnp.einsum(eq, a, b, preferred_element_type=jnp.float32) * scale  7.53 us

commit v1 on v0

--- a/solution.py
+++ b/solution.py
@@ -492,35 +492,32 @@
     )(slots, tok, cot, length, vec, *shards_in)
 
 
-def add_into(dst, left, parts, rows):
-    def go(i, carry):
-        at = pl.ds(pl.multiple_of(i * rows, rows), rows)
-        total = left[at, :].astype(jnp.float32)
-        for part in parts:
-            total = total + part[at, :].astype(jnp.float32)
-        dst[at, :] = total.astype(dst.dtype)
-        return carry
-
-    lax.fori_loop(0, dst.shape[0] // rows, go, 0)
-
-
-def reduce_kernel(rep_size, fsdp_size, weights, *refs):
+LOADED = 17
+
+
+def backward_kernel(rep_size, fsdp_size, weights, *refs):
     F = fsdp_size
     refs = list(refs)
     take = lambda k: [refs.pop(0) for _ in range(k)]
-    res, gin = take(2)
-    grads = take(weights)
-    ores, ogin = take(2)
+    res, prob = take(2)
+    given = take(LOADED)
+    inv1, inv2, kept_in, vec_in = take(4)
+    ores, ogin, gin = take(3)
     owned = take(weights)
+    have = take(LOADED)
+    (w_outer, w_inner, w_out, w_query, w_key, w_value, x_v, seed_v, query_v, key_v, value_v,
+     context_v, norm1_v, norm2_v, low_v, act_v, slope_v) = have
+    inv1_v, inv2_v, kept_v, vec_v, par_v = take(5)
+    prob_v, gf_v, ga_v, gc_v, gq_v, gk_v, gv_v, gin_v, sum_v, sum_in_v, table_v = take(11)
     half_in = take(weights)
-    half_own = take(weights)
+    half_out = take(weights)
     quad_in = take(weights)
     quad_sum = take(weights)
     line_in = take(weights)
     line_sum = take(weights)
     group_count = rep_size // (2 * QUAD)
     group_in = take(weights) if group_count > 1 else None
-    xs, xr, ys, yr, ps, pr, qs, qr, zs, zr, gs, gr, hs, hr, bs, br, own = take(17)
+    xs, xr, ys, yr, ps, pr, qs, qr, zs, zr, gs, gr, hs, hr, bs, br, own, load_sem, prob_sem = take(19)
     r, f, core, chip, q, base = position(F)
     count = rep_size * F
     me = r * F + f
@@ -535,14 +532,14 @@
         return {"rep": (base + lax.rem(q + m, QUAD)) * 2 + core, "fsdp": f}
 
     def columns(ref, w, which):
-        half = grads[w].shape[1] // 2
+        half = half_in[w].shape[1]
         return ref.at[:, pl.ds(pl.multiple_of(which * half, half), half)]
 
     def swap(w):
-        return remote(columns(grads[w], w, 1 - core), half_in[w], ps.at[w], pr.at[w], partner)
+        return remote(half_out[w], half_in[w], ps.at[w], pr.at[w], partner)
 
     def size(w):
-        S = grads[w].shape[0] // F
+        S = half_in[w].shape[0] // F
         return S, S // QUAD
 
     near = (flip(q, 1), flip(q, 2))
@@ -586,7 +583,7 @@
 
     def home(w, quarter, which):
         S, sq = size(w)
-        half = grads[w].shape[1] // 2
+        half = half_in[w].shape[1]
         return owned[w].at[
             pl.ds(pl.multiple_of(quarter * sq, sq), sq), pl.ds(pl.multiple_of(which * half, half), half)
         ]
@@ -602,23 +599,53 @@
         part = columns(owned[w], w, (1 - core) if arriving else core)
         return remote(part, part, bs.at[w], br.at[w], partner)
 
-    for w in range(weights):
+    f32, bf16 = jnp.float32, jnp.bfloat16
+    n_rows, width = x_v.shape
+    wide = slope_v.shape[1]
+    sources = [
+        (act_v, gf_v), (low_v, slope_v), (context_v, ga_v), (x_v, gq_v), (x_v, gk_v), (x_v, gv_v)
+    ]
+    table_at = weights - 1
+
+    def load(k):
+        return pltpu.make_async_copy(given[k], have[k], load_sem.at[k])
+
+    def gradient(w, which, emit):
+        if w == table_at:
+            emit(pl.ds(0, table_v.shape[0]), pl.ds(0, 128),
+                 table_v[:, pl.ds(pl.multiple_of(which * 128, 128), 128)])
+            return
+        left, right = sources[w]
+        half = half_in[w].shape[1]
+        tile = 256
+        span = min(half, 768)
+        across_tiles = half // span
+
+        def go(i, carry):
+            rows_at = pl.ds(pl.multiple_of(lax.div(i, across_tiles) * tile, tile), tile)
+            start = lax.rem(i, across_tiles) * span
+            from_at = pl.ds(pl.multiple_of(which * half + start, 128), span)
+            total = matmul_left_t(left[:, rows_at], right[:, from_at])
+            emit(rows_at, pl.ds(pl.multiple_of(start, 128), span), total)
+            return carry
+
+        lax.fori_loop(0, left.shape[1] // tile * across_tiles, go, 0)
+
+    def offer(w):
+        def emit(rows_at, cols_at, total):
+            half_out[w][rows_at, cols_at] = total.astype(half_out[w].dtype)
+
+        gradient(w, 1 - core, emit)
         swap(w).start()
-    local = [
-        pltpu.make_async_copy(block_of(res, me, rows), block_of(ores, me, rows), own.at[0]),
-        pltpu.make_async_copy(block_of(gin, me, rows), block_of(ogin, me, rows), own.at[1]),
-    ]
-    kept = [
-        pltpu.make_async_copy(columns(grads[w], w, core), half_own[w], own.at[2 + w])
-        for w in range(weights)
-    ]
-    for c in local + kept:
-        c.start()
 
     def step_one(w):
-        kept[w].wait()
         swap(w).wait_recv()
-        add_into(half_in[w], half_in[w], [half_own[w]], size(w)[1])
+
+        def emit(rows_at, cols_at, total):
+            total = total + half_in[w][rows_at, cols_at].astype(f32)
+            half_in[w][rows_at, cols_at] = total.astype(half_in[w].dtype)
+
+        gradient(w, core, emit)
         for t in range(F):
             for k in range(2):
                 across(w, t, k).start()
@@ -667,7 +694,7 @@
     def finish(w):
         for m in range(1, QUAD):
             spread(w, m, False).start()
-        c = pltpu.make_async_copy(line_sum[w], home(w, q, core), own.at[2 + w])
+        c = pltpu.make_async_copy(line_sum[w], home(w, q, core), own.at[5 + w])
         c.start()
         c.wait()
 
@@ -676,14 +703,228 @@
             spread(w, m, True).wait_recv()
         beside(w, False).start()
 
+    row_block = 128
+    blocks = n_rows // row_block
+
+    def sum_rows(k, values):
+        sum_v[k : k + 1, :] = sum_v[k : k + 1, :] + jnp.sum(values, axis=0, keepdims=True)
+
+    def norm_back(grad_out, normed, inv, gain):
+        grad_normed = grad_out * gain
+        first = jnp.mean(grad_normed, axis=-1, keepdims=True)
+        second = jnp.mean(grad_normed * normed, axis=-1, keepdims=True)
+        return (grad_normed - first - normed * second) * inv
+
+    def second_norm():
+        def go(i, carry):
+            at = pl.ds(pl.multiple_of(i * row_block, row_block), row_block)
+            row = lax.broadcasted_iota(jnp.int32, (row_block, 1), 0) + i * row_block
+            live = row < jnp.max(kept_v[1:2, 0:1])
+            seed = jnp.where(live, seed_v[at, :].astype(f32), 0.0)
+            normed = norm2_v[at, :]
+            sum_rows(6, seed * normed)
+            sum_rows(7, seed)
+            grad = norm_back(seed, normed, inv2_v[at, 0:1], par_v[6:7, :])
+            norm2_v[at, :] = grad
+            low = grad.astype(bf16)
+            gf_v[at, :] = low
+            sum_rows(5, low.astype(f32))
+            return carry
+
+        lax.fori_loop(0, blocks, go, 0)
+
+    def through_gelu():
+        tile = 256
+
+        def go(i, carry):
+            at = pl.ds(pl.multiple_of(i * tile, tile), tile)
+            grad = matmul_right_t(gf_v[...], w_outer[at, :])
+            low = (grad * slope_v[:, at].astype(f32)).astype(bf16)
+            slope_v[:, at] = low
+            sum_in_v[0:1, at] = jnp.sum(low.astype(f32), axis=0, keepdims=True)
+            return carry
+
+        lax.fori_loop(0, wide // tile, go, 0)
+
+    def first_norm():
+        def go(i, carry):
+            at = pl.ds(pl.multiple_of(i * row_block, row_block), row_block)
+            grad = norm2_v[at, :] + matmul_right_t(slope_v[at, :], w_inner[...])
+            normed = norm1_v[at, :]
+            sum_rows(3, grad * normed)
+            sum_rows(4, grad)
+            grad = norm_back(grad, normed, inv1_v[at, 0:1], par_v[3:4, :])
+            norm2_v[at, :] = grad
+            low = grad.astype(bf16)
+            ga_v[at, :] = low
+            sum_rows(2, low.astype(f32))
+            return carry
+
+        lax.fori_loop(0, blocks, go, 0)
+
+    def through_out():
+        tile = 256
+
+        def go(i, carry):
+            at = pl.ds(pl.multiple_of(i * tile, tile), tile)
+            gc_v[:, at] = matmul_right_t(ga_v[...], w_out[at, :]).astype(bf16)
+            return carry
+
+        lax.fori_loop(0, width // tile, go, 0)
+
+    def prob_load(pair):
+        slot = lax.rem(pair, 2)
+        return pltpu.make_async_copy(prob.at[pl.ds(pair * 2, 2)], prob_v.at[slot], prob_sem.at[slot])
+
+    pairs = width // 128
+    scale = HD ** (-0.5)
+
+    def attend_back(first, last):
+        def go(pair, carry):
+            prob_load(pair).wait()
+
+            @pl.when(pair + 1 < pairs)
+            def _():
+                prob_load(pair + 1).start()
+
+            slot = lax.rem(pair, 2)
+            lanes = pl.ds(pl.multiple_of(pair * 128, 128), 128)
+            block = 256
+            lane = lax.broadcasted_iota(jnp.int32, (n_rows, 128), 1)
+            keys, values = key_v[:, lanes], value_v[:, lanes]
+            zero = jnp.zeros_like(keys)
+            grad_key = jnp.zeros((n_rows, 128), f32)
+            grad_value = jnp.zeros((n_rows, 128), f32)
+            for start in range(0, n_rows, block):
+                queries = query_v[start : start + block, lanes]
+                grads = gc_v[start : start + block, lanes]
+                grad_query = jnp.zeros((block, 128), f32)
+                for side in range(2):
+                    mine = (lane >= side * HD) & (lane < side * HD + HD)
+                    part = mine[:block]
+                    chance = prob_v[slot, side, start : start + block, :]
+                    wide_chance = chance.astype(f32)
+                    grad_prob = matmul_right_t(grads, jnp.where(mine, values, zero))
+                    centered = jnp.sum(wide_chance * grad_prob, axis=-1, keepdims=True)
+                    grad_score = (wide_chance * (grad_prob - centered)).astype(bf16)
+                    grad_query = grad_query + jnp.dot(
+                        grad_score, jnp.where(mine, keys, zero), preferred_element_type=f32
+                    )
+                    grad_key = grad_key + matmul_left_t(
+                        grad_score, jnp.where(part, queries, zero[:block])
+                    )
+                    grad_value = grad_value + matmul_left_t(
+                        chance, jnp.where(part, grads, zero[:block])
+                    )
+                gq_v[start : start + block, lanes] = (grad_query * scale).astype(bf16)
+            gk_v[:, lanes] = (grad_key * scale).astype(bf16)
+            gv_v[:, lanes] = grad_value.astype(bf16)
+            return carry
+
+        lax.fori_loop(first, last, go, 0)
+
+    def input_grad():
+        def go(i, carry):
+            at = pl.ds(pl.multiple_of(i * row_block, row_block), row_block)
+            total = norm2_v[at, :] + matmul_right_t(gq_v[at, :], w_query[...])
+            total = total + matmul_right_t(gk_v[at, :], w_key[...])
+            total = total + matmul_right_t(gv_v[at, :], w_value[...])
+            gin_v[at, :] = total.astype(bf16)
+            sum_rows(0, gq_v[at, :].astype(f32))
+            sum_rows(1, gv_v[at, :].astype(f32))
+            return carry
+
+        lax.fori_loop(0, blocks, go, 0)
+
+    def fill_table():
+        table_v[...] = jnp.zeros_like(table_v)
+        each = table_v.shape[0] // F
+        thin, part = width // F, wide // F
+        for t in range(F):
+            table_v[t * each : t * each + 8, 0:thin] = sum_v[0:8, :][:, t * thin : (t + 1) * thin]
+            for k in range(part // 128):
+                table_v[t * each + 8 + k : t * each + 9 + k, 0:128] = (
+                    sum_in_v[0:1, t * part + k * 128 : t * part + (k + 1) * 128]
+                )
+
     steps = [step_one, step_turn, step_two, step_three] + ([step_group] if group_count > 1 else []) + [step_four]
-    for at in range(weights + len(steps) - 1):
-        for k, step in enumerate(steps):
-            if 0 <= at - k < weights:
-                step(at - k)
-        if at == 0:
-            trade_res.start()
-            trade_gin.start()
+    done = [0] * weights
+
+    def run(*ws):
+        for w in ws:
+            if done[w] < len(steps):
+                steps[done[w]](w)
+                done[w] += 1
+
+    trade_res.start()
+    small = [
+        pltpu.make_async_copy(a, b, own.at[1 + k])
+        for k, (a, b) in enumerate(
+            ((inv1, inv1_v), (inv2, inv2_v), (kept_in, kept_v), (vec_in, vec_v))
+        )
+    ]
+    keep_res = pltpu.make_async_copy(block_of(res, me, rows), block_of(ores, me, rows), own.at[0])
+    keep_res.start()
+    for c in small:
+        c.start()
+    for k in (7, 13, 15, 0, 16, 14, 1, 12, 11, 2, 8, 9, 10, 6, 3, 4, 5):
+        load(k).start()
+    prob_load(0).start()
+    sum_v[...] = jnp.zeros_like(sum_v)
+    sum_in_v[...] = jnp.zeros_like(sum_in_v)
+    for c in small:
+        c.wait()
+    narrow = jnp.zeros((8, width), f32)
+    vrows = vec_v.shape[0] // F
+    for k in range(F):
+        narrow = narrow + vec_v[k * vrows : k * vrows + 16, :].astype(f32)[0:8, :]
+    par_v[...] = narrow
+    for k in (7, 13):
+        load(k).wait()
+    second_norm()
+    load(15).wait()
+    offer(0)
+    for k in (0, 16):
+        load(k).wait()
+    through_gelu()
+    run(0)
+    load(14).wait()
+    offer(1)
+    for k in (1, 12):
+        load(k).wait()
+    first_norm()
+    run(0, 1)
+    for k in (11, 2):
+        load(k).wait()
+    offer(2)
+    through_out()
+    for k in (8, 9, 10):
+        load(k).wait()
+    attend_back(0, pairs // 3)
+    run(0, 2)
+    attend_back(pairs // 3, 2 * pairs // 3)
+    run(1, 0)
+    attend_back(2 * pairs // 3, pairs)
+    load(6).wait()
+    for w in (3, 4, 5):
+        offer(w)
+    run(2, 1)
+    for k in (3, 4, 5):
+        load(k).wait()
+    input_grad()
+    put = pltpu.make_async_copy(gin_v, gin, load_sem.at[LOADED])
+    put.start()
+    fill_table()
+    offer(table_at)
+    put.wait()
+    keep_gin = pltpu.make_async_copy(block_of(gin, me, rows), block_of(ogin, me, rows), own.at[0])
+    keep_res.wait()
+    trade_gin.start()
+    keep_gin.start()
+    local = [keep_gin]
+    run(3, 4, 5, 6)
+    while min(done) < len(steps):
+        run(*range(weights))
     for w in range(weights):
         beside(w, True).wait_recv()
         swap(w).wait_send()
@@ -702,39 +943,50 @@
     trade_gin.wait()
 
 
-def reduce_all(rep_size, fsdp_size, res, gin, grads):
-    weights = len(grads)
+def backward(rep_size, fsdp_size, res, prob, given, inv1, inv2, kept, vec):
     count = rep_size * fsdp_size
     F = fsdp_size
     groups = rep_size // (2 * QUAD)
     like = jax.ShapeDtypeStruct
+    bf16, f32 = jnp.bfloat16, jnp.float32
     anywhere = pl.BlockSpec(memory_space=pl.ANY)
-    outs = [like(res.shape, res.dtype), like(gin.shape, gin.dtype)] + [
+    n_rows, width = res.shape
+    grads = [like(w.shape, bf16) for w in given[:6]] + [like((F * 32, 256), f32)]
+    weights = len(grads)
+    outs = [like(res.shape, res.dtype)] * 3 + [
         like((g.shape[0] // F, g.shape[1]), g.dtype) for g in grads
     ]
     V = pltpu.VMEM
-    scratch = [V((g.shape[0], g.shape[1] // 2), g.dtype) for g in grads]
-    scratch += [V((g.shape[0], g.shape[1] // 2), g.dtype) for g in grads]
-    scratch += [V((3, F, g.shape[0] // QUAD // F, g.shape[1] // 2), g.dtype) for g in grads]
-    scratch += [V((g.shape[0] // QUAD, g.shape[1] // 2), g.dtype) for g in grads]
-    scratch += [V((F - 1, g.shape[0] // QUAD // F, g.shape[1] // 2), g.dtype) for g in grads]
-    scratch += [V((g.shape[0] // QUAD // F, g.shape[1] // 2), g.dtype) for g in grads]
+    halves = [(g.shape[0], g.shape[1] // 2, g.dtype) for g in grads]
+    rows_of = lambda columns, kind: V((n_rows, columns), kind)
+    scratch = [V(a.shape, a.dtype) for a in list(given) + [inv1, inv2, kept, vec]]
+    scratch += [V((8, width), f32), V((2, 2, n_rows, n_rows), bf16)]
+    scratch += [rows_of(width, bf16)] * 7
+    scratch += [V((8, width), f32), V((8, given[1].shape[1]), f32), V((F * 32, 256), f32)]
+    scratch += [V((r, c), d) for r, c, d in halves]
+    scratch += [V((r, c), d) for r, c, d in halves]
+    scratch += [V((3, F, r // QUAD // F, c), d) for r, c, d in halves]
+    scratch += [V((r // QUAD, c), d) for r, c, d in halves]
+    scratch += [V((F - 1, r // QUAD // F, c), d) for r, c, d in halves]
+    scratch += [V((r // QUAD // F, c), d) for r, c, d in halves]
     if groups > 1:
-        scratch += [V((groups - 1, g.shape[0] // QUAD // F, g.shape[1] // 2), g.dtype) for g in grads]
+        scratch += [V((groups - 1, r // QUAD // F, c), d) for r, c, d in halves]
     scratch += [DMA((count,))] * 4 + [DMA((weights,))] * 2 + [DMA((weights, F, 3))] * 2
     scratch += [DMA((weights, F))] * 2 + [DMA((weights, max(groups, 2)))] * 2
-    scratch += [DMA((weights, QUAD))] * 2 + [DMA((weights,))] * 2 + [DMA((2 + weights,))]
-    return pl.pallas_call(
-        functools.partial(reduce_kernel, rep_size, fsdp_size, weights),
+    scratch += [DMA((weights, QUAD))] * 2 + [DMA((weights,))] * 2 + [DMA((5 + weights,))]
+    scratch += [DMA((LOADED + 1,)), DMA((2,))]
+    outs_all = pl.pallas_call(
+        functools.partial(backward_kernel, rep_size, fsdp_size, weights),
         out_shape=outs,
-        in_specs=[anywhere] * (2 + weights),
-        out_specs=[anywhere] * (2 + weights),
+        in_specs=[anywhere] * (6 + LOADED),
+        out_specs=[anywhere] * len(outs),
         scratch_shapes=scratch,
         compiler_params=pltpu.CompilerParams(
-            collective_id=2, has_side_effects=True, vmem_limit_bytes=56 * 2**20
+            collective_id=2, has_side_effects=True, vmem_limit_bytes=67043328
         ),
-        name="reduce_all",
-    )(res, gin, *grads)
+        name="backward",
+    )(res, prob, *given, inv1, inv2, kept, vec)
+    return outs_all[0], outs_all[1], outs_all[3:]
 
 
 def widen_kernel(count, *refs):
@@ -772,13 +1024,6 @@
     return lax.dot_general(
         left, right, (((1,), (1,)), ((), ())), preferred_element_type=jnp.float32
     )
-
-
-def norm_backward(grad_out, normed, scaled_inv, norm_gain):
-    grad_normed = grad_out * norm_gain
-    first_mean = jnp.mean(grad_normed, axis=-1, keepdims=True)
-    second_mean = jnp.mean(grad_normed * normed, axis=-1, keepdims=True)
-    return (grad_normed - first_mean - normed * second_mean) * scaled_inv
 
 
 def shards(
@@ -807,8 +1052,6 @@
     row_count, feature_dim = tokens.shape
     small = [query_bias, value_bias, out_bias, first_gain, first_shift, outer_bias, second_gain, second_shift]
     width = query_bias.shape[0]
-    wide = inner_bias.shape[0] // width
-    lanes = 256
     vec_rows = 16
     chosen = jnp.arange(fsdp_size, dtype=jnp.int32) == lax.axis_index("fsdp")
 
@@ -827,81 +1070,16 @@
         rep_size, fsdp_size, slot_seq, tokens, cotangent, length_block, vec,
         [query_weight, key_weight, value_weight, out_weight, inner_weight, outer_weight],
     )
-    kept = kept_table[0] > 0
-    params = all_vec.reshape(fsdp_size, vec_rows, feature_dim)[:, :8].astype(jnp.float32).sum(axis=0)
-    first_gain_full, second_gain_full = params[3], params[6]
-    first_inv, second_inv = first_inv[:, :1], second_inv[:, :1]
-    head_shape = (row_count, HEADS, HD)
-    seed_rows = jnp.where(kept[:, None], seq_seed.astype(jnp.float32), 0.0)
-    grad_second_gain = jnp.sum(seed_rows * second_normed, axis=0)
-    grad_second_shift = jnp.sum(seed_rows, axis=0)
-    grad_second = norm_backward(seed_rows, second_normed, second_inv, second_gain_full)
-    grad_outer = grad_second.astype(jnp.bfloat16)
-    grad_outer_bias = jnp.sum(grad_outer, axis=0, dtype=jnp.float32)
-    grad_outer_weight = matmul_left_t(activated, grad_outer)
-    grad_activated = matmul_right_t(grad_outer, outer_full)
-    grad_inner = (grad_activated * slope).astype(jnp.bfloat16)
-    grad_inner_bias = jnp.sum(grad_inner, axis=0, dtype=jnp.float32)
-    grad_inner_weight = matmul_left_t(hidden_low, grad_inner)
-    grad_hidden = grad_second + matmul_right_t(grad_inner, inner_full)
-    grad_first_gain = jnp.sum(grad_hidden * first_normed, axis=0)
-    grad_first_shift = jnp.sum(grad_hidden, axis=0)
-    grad_residual = norm_backward(grad_hidden, first_normed, first_inv, first_gain_full)
-    grad_attended = grad_residual.astype(jnp.bfloat16)
-    grad_out_bias = jnp.sum(grad_attended, axis=0, dtype=jnp.float32)
-    grad_out_weight = matmul_left_t(context, grad_attended)
-    grad_context = matmul_right_t(grad_attended, out_full).astype(jnp.bfloat16)
-    heads_of = lambda a: a.reshape(head_shape)
-    grad_rows_h = heads_of(grad_context)
-    prob32 = probs.astype(jnp.float32)
-    grad_prob = jnp.einsum(
-        "qhd,khd->hqk", grad_rows_h, heads_of(value_rows), preferred_element_type=jnp.float32
-    )
-    centered = jnp.sum(prob32 * grad_prob, axis=-1, keepdims=True)
-    grad_scores = (prob32 * (grad_prob - centered)).astype(jnp.bfloat16)
-    back = lambda eq, a, b, scale: (
-        (jnp.einsum(eq, a, b, preferred_element_type=jnp.float32) * scale)
-        .astype(jnp.bfloat16).reshape(row_count, feature_dim)
-    )
-    scale = HD ** (-0.5)
-    grad_query = back("hqk,khd->qhd", grad_scores, heads_of(key_rows), scale)
-    grad_key = back("hqk,qhd->khd", grad_scores, heads_of(query_rows), scale)
-    grad_value = back("hqk,qhd->khd", probs, grad_rows_h, 1.0)
-    grad_query_bias = jnp.sum(grad_query, axis=0, dtype=jnp.float32)
-    grad_value_bias = jnp.sum(grad_value, axis=0, dtype=jnp.float32)
-    grad_query_weight = matmul_left_t(seq_rows, grad_query)
-    grad_key_weight = matmul_left_t(seq_rows, grad_key)
-    grad_value_weight = matmul_left_t(seq_rows, grad_value)
-    grad_input = (
-        grad_residual
-        + matmul_right_t(grad_query, query_full)
-        + matmul_right_t(grad_key, key_full)
-        + matmul_right_t(grad_value, value_full)
-    ).astype(jnp.bfloat16)
-    low = lambda g: g.astype(jnp.bfloat16)
-    grad_small = [
-        grad_query_bias, grad_value_bias, grad_out_bias, grad_first_gain, grad_first_shift,
-        grad_outer_bias, grad_second_gain, grad_second_shift,
-    ]
-    grad_table = jnp.concatenate(
+    back_rows, back_grads, (
+        d_outer, d_inner, d_out, d_query, d_key, d_value, d_vec,
+    ) = backward(
+        rep_size, fsdp_size, result, probs,
         [
-            jnp.stack(grad_small).reshape(8, fsdp_size, width).transpose(1, 0, 2),
-            grad_inner_bias.reshape(fsdp_size, wide, width),
+            outer_full, inner_full, out_full, query_full, key_full, value_full,
+            seq_rows, seq_seed, query_rows, key_rows, value_rows, context,
+            first_normed, second_normed, hidden_low, activated, slope,
         ],
-        axis=1,
-    )
-    grad_rows = 32
-    grad_table = jnp.pad(
-        grad_table, ((0, 0), (0, grad_rows - 8 - wide), (0, lanes - width))
-    ).reshape(fsdp_size * grad_rows, lanes)
-    (
-        back_rows, back_grads, d_outer, d_inner, d_out, d_query, d_key, d_value, d_vec,
-    ) = reduce_all(
-        rep_size, fsdp_size, result, grad_input,
-        [
-            low(grad_outer_weight), low(grad_inner_weight), low(grad_out_weight),
-            low(grad_query_weight), low(grad_key_weight), low(grad_value_weight), grad_table,
-        ],
+        first_inv, second_inv, kept_table, all_vec,
     )
     d_outer, d_inner, d_out, d_query, d_key, d_value = widen(
         [d_outer, d_inner, d_out, d_query, d_key, d_value]
@@ -910,7 +1088,7 @@
     return (
         back_rows, back_grads,
         d_query, v[0], d_key, d_value, v[1], d_out, v[2], v[3], v[4],
-        d_inner, v[8 : 8 + wide].reshape(-1), d_outer, v[5], v[6], v[7],
+        d_inner, d_vec[8 : 8 + inner_bias.shape[0] // 128, :128].reshape(-1), d_outer, v[5], v[6], v[7],
     )
 
 

time: 322 us -> 266 us (0.83)
  matrix products: 42.5 us -> 0 us
  local copies, waits for them, and re-layouts: 19.8 us -> 7.8 us
  other arithmetic: 6.9 us -> 0.85 us
  Pallas kernels: 251 us -> 256 us
    dot_general x16 -> x0, matrix products: 42.5 us -> none  [the longest x6 16.1 us: matmul_left_t(): lax.dot_general(left, right, (((0,), (0,)), ((), ())), preferred_element_...]
    pallas_call x3 -> x0, local copies, waits for them, and re-layouts: 5.39 us -> none  [fetch(): pl.pallas_call(functools.partial(fetch_kernel, rep_size, fsdp_size, weigh...]
    pallas_call x1, Pallas kernels: 122 us -> 127 us  [backward(): pl.pallas_call(functools.partial(backward_kernel, rep_size, fsdp_size, we...]
    unnamed x64 -> x6, local copies, waits for them, and re-layouts: 6.4 us -> 2.29 us
where the time goes in v1:
time: 266 us
  Pallas kernels  256 us (96%)
  local copies, waits for them, and re-layouts  7.8 us (3%)
    pallas_call x1, Pallas kernels, backward(): pl.pallas_call(functools.partial(backward_kernel, rep_size, fsdp_size, we...  127 us
    pallas_call x1, Pallas kernels, fetch(): pl.pallas_call(functools.partial(fetch_kernel, rep_size, fsdp_size, weigh...  124 us

profile of v1, /device:TPU:0, one launch (start us, length us, event | category | flops | bytes accessed | tf_op | source)
XLA Modules:
  0.0 265.6 jit_solution(8242149994668655047)
XLA Ops:
  1.3 0.7 stack.6
  2.0 0.6 broadcast_in_dim.125.refs_3_
  2.6 0.8 broadcast_select_fusion
  3.4 0.1 select_n.120
  3.5 0.1 select_n.108
  3.6 0.1 select_n.110
  3.7 0.1 select_n.112
  3.8 0.1 select_n.114
  3.9 0.1 select_n.116
  4.0 0.1 select_n.118
  4.0 0.1 select_n.106
  4.1 0.1 stack.7
  4.2 0.6 pad.4.refs_4_
  4.8 123.6 %forward.1 = (bf16[512,768]{1,0:T(8,128)(2,1)}, bf16[512,768]{1,0:T(8,128)(2,1)}, bf16[64,768]{1,0:T(8,128)(2,1)}, bf16[768,768]{1,0:T(8,128)(2,1)}, bf16[768,76...) custom-call(s32[32]{0:T(128)} %refs_0_.1, ...), custom_call_target="tpu_custom_call" | custom-call | tf_op jit(solution)/shard_map/forward/pallas_call | solution.py:472
  128.5 126.6 %backward.1 = (bf16[512,768]{1,0:T(8,128)(2,1)}, bf16[512,768]{1,0:T(8,128)(2,1)}, bf16[512,768]{1,0:T(8,128)(2,1)}, bf16[768,768]{1,0:T(8,128)(2,1)}, bf16[192,...) custom-call(bf16[512,768]{1,0:T(8,128)(2,1)} %get-tuple-element.55.r, ...), custom_call_target="tpu_custom_call" | custom-call | tf_op jit(solution)/shard_map/backward/pallas_call | solution.py:978
  255.1 1.3 slice_bitcast_fusion
  256.4 1.6 fusion
  258.0 0.0 copy-start.1
  258.0 5.3 %widen.1 = (f32[768,768]{1,0:T(8,128)}, f32[192,3072]{1,0:T(8,128)}, f32[192,768]{1,0:T(8,128)}, f32[192,768]{1,0:T(8,128)}, f32[192,768]{1,0:T(8,128)}, /*index=5*/f32[192,768]{1,0:T(8,128)}) custom-call(bf16[768,768]{1,0:T(8,128)(2,1)} %get-tuple-element.80.refs_0_, bf16[192,3072]{1,0:T(8,128)(2,1)} %get-tuple-element.81.refs_1_, ...), custom_call_target="tpu_custom_call" | custom-call | tf_op jit(solution)/shard_map/widen/pallas_call | solution.py:1003
  263.3 0.0 copy-start
  263.3 0.0 copy-done.1
  263.3 0.9 copy.39
  264.2 0.5 copy-done
  264.7 0.9 copy.40
  (1 shorter events, 0.0 us)
Async XLA Ops:
  258.0 5.3 %copy-start.1 = (bf16[512,768]{1,0:T(8,128)(2,1)S(1)}, bf16[512,768]{1,0:T(8,128)(2,1)}, u32[]{:S(2)}) copy-start(bf16[512,768]{1,0:T(8,128)(2,1)} %get-tuple-element.126) | copy-start | bytes 2359300
  263.3 1.4 copy-start
